TPU v7x, 8 devices: a whole 2x2x1 slice. The times are simulated.
8 devices in a mesh: rep: 1 (over z), pp: 8 (over x, y, core).
Axes of the slice: x: 2, y: 2, z: 1, core: 2. Of those that a mesh axis runs over, the one named last changes fastest.
Arguments:
- x: bfloat16 [16, 512, 640], P('rep')
- dy: bfloat16 [16, 512, 640], P('rep')
- w_gate: bfloat16 [8, 640, 1536], P('pp')
- w_up: bfloat16 [8, 640, 1536], P('pp')
- w_down: bfloat16 [8, 1536, 640], P('pp')
Outputs:
- output 1: bfloat16 [8, 640, 1536], P(('rep', 'pp'))
- output 2: bfloat16 [8, 640, 1536], P(('rep', 'pp'))
- output 3: bfloat16 [8, 1536, 640], P(('rep', 'pp'))
All inputs are finite; a program needn't handle non-finite values.
Results may differ from a plain program's by a relative error of at most 0.0288.
Values are sent between devices in bfloat16 or wider.
A program may use at most 2 GiB of HBM per device.

v0:
```python
import jax
import jax.numpy as jnp
from jax import lax
from jax.sharding import PartitionSpec as P

NAMES = ("w_gate", "w_up", "w_down")


def matmul(a, w):
    return jnp.dot(a, w, preferred_element_type=jnp.float32).astype(jnp.bfloat16)


def normed(h):
    wide = h.astype(jnp.float32)
    scale = lax.rsqrt(jnp.mean(wide**2, -1, keepdims=True) + 1e-6)
    return (wide * scale).astype(jnp.bfloat16)


def layer(h, w):
    a = normed(h)
    gate = jnp.dot(a, w["w_gate"], preferred_element_type=jnp.float32)
    up = jnp.dot(a, w["w_up"], preferred_element_type=jnp.float32)
    return h + matmul((jax.nn.silu(gate) * up).astype(jnp.bfloat16), w["w_down"])


def stage(weights, h):
    for number in range(weights["w_gate"].shape[0]):
        h = layer(h, {name: w[number] for name, w in weights.items()})
    return h


def solution(mesh):
    stages = mesh.shape["pp"]
    onward = [(i, i + 1) for i in range(stages - 1)]
    back_again = [(i + 1, i) for i in range(stages - 1)]

    def step(x, dy, *arrays):
        weights = dict(zip(NAMES, arrays, strict=True))
        micro, me = x.shape[0], lax.axis_index("pp")
        kept, came = jnp.zeros_like(x), jnp.zeros_like(x[0])
        for t in range(micro + stages - 1):
            number = jnp.clip(t - me, 0, micro - 1)
            at_work = (t >= me) & (t - me < micro)
            h = jnp.where(me == 0, x[min(t, micro - 1)], came)
            was = lax.dynamic_index_in_dim(kept, number, 0, keepdims=False)
            kept = lax.dynamic_update_index_in_dim(kept, jnp.where(at_work, h, was), number, 0)
            came = lax.ppermute(stage(weights, h), "pp", onward)
        total = {name: jnp.zeros(w.shape, jnp.float32) for name, w in weights.items()}
        came, behind = jnp.zeros_like(x[0]), stages - 1 - me
        for t in range(micro + stages - 1):
            number = jnp.clip(t - behind, 0, micro - 1)
            at_work = (t >= behind) & (t - behind < micro)
            by_y = jnp.where(behind == 0, dy[min(t, micro - 1)], came)
            _, back = jax.vjp(stage, weights, lax.dynamic_index_in_dim(kept, number, 0, keepdims=False))
            by_w, by_h = back(by_y)
            total = {name: total[name] + jnp.where(at_work, by_w[name].astype(jnp.float32), 0.0) for name in NAMES}
            came = lax.ppermute(by_h, "pp", back_again)
        return tuple(total[name].astype(jnp.bfloat16) for name in NAMES)

    return jax.shard_map(
        step,
        mesh=mesh,
        in_specs=(P("rep", None, None),) * 2 + (P("pp", None, None),) * 3,
        out_specs=(P(("rep", "pp"), None, None),) * 3,
        check_vma=False,
    )
```

profile of v0, /device:TPU:5, one launch (start us, length us, event | category | flops | bytes accessed | tf_op | source)
XLA Modules:
  0.0 1262.7 jit_solution(12127047815936165918)
XLA Ops:
  16.2 7.5 collective-permute-done
  39.3 7.5 collective-permute-done.1
  709.6 7.9 collective-permute-done.25
  735.5 7.7 collective-permute-done.26
  761.0 7.9 collective-permute-done.27
  787.0 7.9 collective-permute-done.28
  813.3 7.7 collective-permute-done.29
  839.1 7.9 collective-permute-done.30
  865.2 7.9 collective-permute-done.31
  891.3 7.8 collective-permute-done.32
  917.1 8.0 collective-permute-done.33
  943.3 7.9 collective-permute-done.34
  969.4 7.8 collective-permute-done.35
  995.3 8.0 collective-permute-done.36
  1021.4 7.9 collective-permute-done.37
  1047.5 7.7 collective-permute-done.38
  1073.3 8.0 collective-permute-done.39
  1099.4 7.8 collective-permute-done.40
  1125.5 7.7 collective-permute-done.41
  1151.3 8.0 collective-permute-done.42
  1183.8 7.9 collective-permute-done.43
  1194.4 21.6 %fusion.94 = bf16[1,640,1536]{2,1,0:T(8,128)(2,1)} fusion(bf16[512,1536]{1,0:T(8,128)(2,1)} %convolution_convert_fusion.69, bf16[640,1536]{1,0:T(8,128)(2,1)} %convolution_convert_fusion.1, bf16[640,1536]{1,0:T(8,128)(2,1)} %convolution_convert_fusion.2, bf16[640,1536]{1,0:T(8,128)(2,1)} %convolution_convert_fusion.3, ...), kind=kOutput, calls=%fused_computation.325 | convolution fusion | flops 1081147392 | bytes 50595868 | tf_op jit(solution)/shard_map/transpose(jvp())/dot_general | solution.py:22
  1216.1 23.4 %fusion.96 = bf16[1,640,1536]{2,1,0:T(8,128)(2,1)} fusion(f32[512,1536]{1,0:T(8,128)} %fusion.278, f32[512,1536]{1,0:T(8,128)} %fusion.188, bf16[512,1536]{1,0:T(8,128)(2,1)} %convolution_convert_fusion.69, bf16[640,1536]{1,0:T(8,128)(2,1)} %convolution_convert_fusion.24, bf16[640,1536]{1,0:T(8,128)(2,1)} %convolution_convert_fusion.25, ...), kind=kOutput, calls=%fused_computation.327 | convolution fusion | flops 1085079552 | bytes 53741596 | tf_op jit(solution)/shard_map/transpose(jvp())/dot_general | solution.py:21
  1239.4 22.7 %fusion.95 = bf16[1,1536,640]{2,1,0:T(8,128)(2,1)} fusion(bf16[1536,640]{1,0:T(8,128)(2,1)} %convolution_convert_fusion.47, bf16[1536,640]{1,0:T(8,128)(2,1)} %convolution_convert_fusion.48, bf16[1536,640]{1,0:T(8,128)(2,1)} %convolution_convert_fusion.49, bf16[1536,640]{1,0:T(8,128)(2,1)} %convolution_convert_fusion.50, ...), kind=kOutput, calls=%fused_computation.326 | convolution fusion | flops 1080492032 | bytes 52822040 | tf_op jit(solution)/shard_map/transpose(jvp())/dot_general | solution.py:10
  (739 shorter events, 1026.4 us)
Async XLA Ops:
  57.1 12.8 %collective-permute-start.2 = (bf16[512,640]{1,0:T(8,128)(2,1)S(1)}, bf16[512,640]{1,0:T(8,128)(2,1)S(1)}, u32[]{:S(2)}, u32[]{:S(2)}) collective-permute-start(bf16[512,640]{1,0:T(8,128)(2,1)S(1)} %fusion.935), channel_id=1, source_target_pairs={{0,1},{1,2},{2,3},{3,4},{4,5},{5,6},{6,7}} | collective-permute-start | bytes 1966088 | tf_op jit(solution)/shard_map/ppermute | solution.py:47
  255.3 12.9 %collective-permute-start.10 = (bf16[512,640]{1,0:T(8,128)(2,1)}, bf16[512,640]{1,0:T(8,128)(2,1)}, u32[]{:S(2)}, u32[]{:S(2)}) collective-permute-start(bf16[512,640]{1,0:T(8,128)(2,1)} %fusion.911), channel_id=1, source_target_pairs={{0,1},{1,2},{2,3},{3,4},{4,5},{5,6},{6,7}} | collective-permute-start | bytes 1966088 | tf_op jit(solution)/shard_map/ppermute | solution.py:47
  305.8 12.9 %collective-permute-start.12 = (bf16[512,640]{1,0:T(8,128)(2,1)}, bf16[512,640]{1,0:T(8,128)(2,1)S(1)}, u32[]{:S(2)}, u32[]{:S(2)}) collective-permute-start(bf16[512,640]{1,0:T(8,128)(2,1)} %fusion.905), channel_id=1, source_target_pairs={{0,1},{1,2},{2,3},{3,4},{4,5},{5,6},{6,7}} | collective-permute-start | bytes 1966088 | tf_op jit(solution)/shard_map/ppermute | solution.py:47
  329.8 12.9 %collective-permute-start.13 = (bf16[512,640]{1,0:T(8,128)(2,1)}, bf16[512,640]{1,0:T(8,128)(2,1)S(1)}, u32[]{:S(2)}, u32[]{:S(2)}) collective-permute-start(bf16[512,640]{1,0:T(8,128)(2,1)} %fusion.902), channel_id=1, source_target_pairs={{0,1},{1,2},{2,3},{3,4},{4,5},{5,6},{6,7}} | collective-permute-start | bytes 1966088 | tf_op jit(solution)/shard_map/ppermute | solution.py:47
  354.0 12.9 %collective-permute-start.14 = (bf16[512,640]{1,0:T(8,128)(2,1)}, bf16[512,640]{1,0:T(8,128)(2,1)S(1)}, u32[]{:S(2)}, u32[]{:S(2)}) collective-permute-start(bf16[512,640]{1,0:T(8,128)(2,1)} %fusion.899), channel_id=1, source_target_pairs={{0,1},{1,2},{2,3},{3,4},{4,5},{5,6},{6,7}} | collective-permute-start | bytes 1966088 | tf_op jit(solution)/shard_map/ppermute | solution.py:47
  379.3 12.9 %collective-permute-start.15 = (bf16[512,640]{1,0:T(8,128)(2,1)}, bf16[512,640]{1,0:T(8,128)(2,1)S(1)}, u32[]{:S(2)}, u32[]{:S(2)}) collective-permute-start(bf16[512,640]{1,0:T(8,128)(2,1)} %fusion.896), channel_id=1, source_target_pairs={{0,1},{1,2},{2,3},{3,4},{4,5},{5,6},{6,7}} | collective-permute-start | bytes 1966088 | tf_op jit(solution)/shard_map/ppermute | solution.py:47
  404.6 12.9 %collective-permute-start.16 = (bf16[512,640]{1,0:T(8,128)(2,1)}, bf16[512,640]{1,0:T(8,128)(2,1)S(1)}, u32[]{:S(2)}, u32[]{:S(2)}) collective-permute-start(bf16[512,640]{1,0:T(8,128)(2,1)} %fusion.893), channel_id=1, source_target_pairs={{0,1},{1,2},{2,3},{3,4},{4,5},{5,6},{6,7}} | collective-permute-start | bytes 1966088 | tf_op jit(solution)/shard_map/ppermute | solution.py:47
  429.8 12.9 %collective-permute-start.17 = (bf16[512,640]{1,0:T(8,128)(2,1)}, bf16[512,640]{1,0:T(8,128)(2,1)S(1)}, u32[]{:S(2)}, u32[]{:S(2)}) collective-permute-start(bf16[512,640]{1,0:T(8,128)(2,1)} %fusion.890), channel_id=1, source_target_pairs={{0,1},{1,2},{2,3},{3,4},{4,5},{5,6},{6,7}} | collective-permute-start | bytes 1966088 | tf_op jit(solution)/shard_map/ppermute | solution.py:47
  453.9 12.9 %collective-permute-start.18 = (bf16[512,640]{1,0:T(8,128)(2,1)}, bf16[512,640]{1,0:T(8,128)(2,1)S(1)}, u32[]{:S(2)}, u32[]{:S(2)}) collective-permute-start(bf16[512,640]{1,0:T(8,128)(2,1)} %fusion.887), channel_id=1, source_target_pairs={{0,1},{1,2},{2,3},{3,4},{4,5},{5,6},{6,7}} | collective-permute-start | bytes 1966088 | tf_op jit(solution)/shard_map/ppermute | solution.py:47
  478.0 12.9 %collective-permute-start.19 = (bf16[512,640]{1,0:T(8,128)(2,1)}, bf16[512,640]{1,0:T(8,128)(2,1)S(1)}, u32[]{:S(2)}, u32[]{:S(2)}) collective-permute-start(bf16[512,640]{1,0:T(8,128)(2,1)} %fusion.884), channel_id=1, source_target_pairs={{0,1},{1,2},{2,3},{3,4},{4,5},{5,6},{6,7}} | collective-permute-start | bytes 1966088 | tf_op jit(solution)/shard_map/ppermute | solution.py:47
  568.5 55.1 %collective-permute-start.22 = (bf16[512,640]{1,0:T(8,128)(2,1)S(1)}, bf16[512,640]{1,0:T(8,128)(2,1)S(1)}, u32[]{:S(2)}, u32[]{:S(2)}) collective-permute-start(bf16[512,640]{1,0:T(8,128)(2,1)S(1)} %fusion.1099), channel_id=1, source_target_pairs={{1,0},{2,1},{3,2},{4,3},{5,4},{6,5},{7,6}} | collective-permute-start | bytes 1966088 | tf_op jit(solution)/shard_map/ppermute | solution.py:57
  637.1 14.5 %collective-permute-start.23 = (bf16[512,640]{1,0:T(8,128)(2,1)S(1)}, bf16[512,640]{1,0:T(8,128)(2,1)S(1)}, u32[]{:S(2)}, u32[]{:S(2)}) collective-permute-start(bf16[512,640]{1,0:T(8,128)(2,1)S(1)} %fusion.1098), channel_id=1, source_target_pairs={{1,0},{2,1},{3,2},{4,3},{5,4},{6,5},{7,6}} | collective-permute-start | bytes 1966088 | tf_op jit(solution)/shard_map/ppermute | solution.py:57
  672.8 13.6 %collective-permute-start.24 = (bf16[512,640]{1,0:T(8,128)(2,1)S(1)}, bf16[512,640]{1,0:T(8,128)(2,1)S(1)}, u32[]{:S(2)}, u32[]{:S(2)}) collective-permute-start(bf16[512,640]{1,0:T(8,128)(2,1)S(1)} %fusion.1097), channel_id=1, source_target_pairs={{1,0},{2,1},{3,2},{4,3},{5,4},{6,5},{7,6}} | collective-permute-start | bytes 1966088 | tf_op jit(solution)/shard_map/ppermute | solution.py:57
  704.7 12.8 %collective-permute-start.25 = (bf16[512,640]{1,0:T(8,128)(2,1)S(1)}, bf16[512,640]{1,0:T(8,128)(2,1)S(1)}, u32[]{:S(2)}, u32[]{:S(2)}) collective-permute-start(bf16[512,640]{1,0:T(8,128)(2,1)S(1)} %fusion.1096), channel_id=1, source_target_pairs={{1,0},{2,1},{3,2},{4,3},{5,4},{6,5},{7,6}} | collective-permute-start | bytes 1966088 | tf_op jit(solution)/shard_map/ppermute | solution.py:57
  730.3 12.8 %collective-permute-start.26 = (bf16[512,640]{1,0:T(8,128)(2,1)S(1)}, bf16[512,640]{1,0:T(8,128)(2,1)S(1)}, u32[]{:S(2)}, u32[]{:S(2)}) collective-permute-start(bf16[512,640]{1,0:T(8,128)(2,1)S(1)} %fusion.1095), channel_id=1, source_target_pairs={{1,0},{2,1},{3,2},{4,3},{5,4},{6,5},{7,6}} | collective-permute-start | bytes 1966088 | tf_op jit(solution)/shard_map/ppermute | solution.py:57
  756.1 12.8 %collective-permute-start.27 = (bf16[512,640]{1,0:T(8,128)(2,1)S(1)}, bf16[512,640]{1,0:T(8,128)(2,1)S(1)}, u32[]{:S(2)}, u32[]{:S(2)}) collective-permute-start(bf16[512,640]{1,0:T(8,128)(2,1)S(1)} %fusion.1094), channel_id=1, source_target_pairs={{1,0},{2,1},{3,2},{4,3},{5,4},{6,5},{7,6}} | collective-permute-start | bytes 1966088 | tf_op jit(solution)/shard_map/ppermute | solution.py:57
  782.1 12.8 %collective-permute-start.28 = (bf16[512,640]{1,0:T(8,128)(2,1)S(1)}, bf16[512,640]{1,0:T(8,128)(2,1)S(1)}, u32[]{:S(2)}, u32[]{:S(2)}) collective-permute-start(bf16[512,640]{1,0:T(8,128)(2,1)S(1)} %fusion.1093), channel_id=1, source_target_pairs={{1,0},{2,1},{3,2},{4,3},{5,4},{6,5},{7,6}} | collective-permute-start | bytes 1966088 | tf_op jit(solution)/shard_map/ppermute | solution.py:57
  808.2 12.8 %collective-permute-start.29 = (bf16[512,640]{1,0:T(8,128)(2,1)S(1)}, bf16[512,640]{1,0:T(8,128)(2,1)S(1)}, u32[]{:S(2)}, u32[]{:S(2)}) collective-permute-start(bf16[512,640]{1,0:T(8,128)(2,1)S(1)} %fusion.1092), channel_id=1, source_target_pairs={{1,0},{2,1},{3,2},{4,3},{5,4},{6,5},{7,6}} | collective-permute-start | bytes 1966088 | tf_op jit(solution)/shard_map/ppermute | solution.py:57
  834.2 12.8 %collective-permute-start.30 = (bf16[512,640]{1,0:T(8,128)(2,1)S(1)}, bf16[512,640]{1,0:T(8,128)(2,1)S(1)}, u32[]{:S(2)}, u32[]{:S(2)}) collective-permute-start(bf16[512,640]{1,0:T(8,128)(2,1)S(1)} %fusion.1091), channel_id=1, source_target_pairs={{1,0},{2,1},{3,2},{4,3},{5,4},{6,5},{7,6}} | collective-permute-start | bytes 1966088 | tf_op jit(solution)/shard_map/ppermute | solution.py:57
  860.3 12.8 %collective-permute-start.31 = (bf16[512,640]{1,0:T(8,128)(2,1)S(1)}, bf16[512,640]{1,0:T(8,128)(2,1)S(1)}, u32[]{:S(2)}, u32[]{:S(2)}) collective-permute-start(bf16[512,640]{1,0:T(8,128)(2,1)S(1)} %fusion.1090), channel_id=1, source_target_pairs={{1,0},{2,1},{3,2},{4,3},{5,4},{6,5},{7,6}} | collective-permute-start | bytes 1966088 | tf_op jit(solution)/shard_map/ppermute | solution.py:57
  886.3 12.8 %collective-permute-start.32 = (bf16[512,640]{1,0:T(8,128)(2,1)S(1)}, bf16[512,640]{1,0:T(8,128)(2,1)S(1)}, u32[]{:S(2)}, u32[]{:S(2)}) collective-permute-start(bf16[512,640]{1,0:T(8,128)(2,1)S(1)} %fusion.1089), channel_id=1, source_target_pairs={{1,0},{2,1},{3,2},{4,3},{5,4},{6,5},{7,6}} | collective-permute-start | bytes 1966088 | tf_op jit(solution)/shard_map/ppermute | solution.py:57
  912.3 12.8 %collective-permute-start.33 = (bf16[512,640]{1,0:T(8,128)(2,1)S(1)}, bf16[512,640]{1,0:T(8,128)(2,1)S(1)}, u32[]{:S(2)}, u32[]{:S(2)}) collective-permute-start(bf16[512,640]{1,0:T(8,128)(2,1)S(1)} %fusion.1088), channel_id=1, source_target_pairs={{1,0},{2,1},{3,2},{4,3},{5,4},{6,5},{7,6}} | collective-permute-start | bytes 1966088 | tf_op jit(solution)/shard_map/ppermute | solution.py:57
  938.4 12.8 %collective-permute-start.34 = (bf16[512,640]{1,0:T(8,128)(2,1)S(1)}, bf16[512,640]{1,0:T(8,128)(2,1)S(1)}, u32[]{:S(2)}, u32[]{:S(2)}) collective-permute-start(bf16[512,640]{1,0:T(8,128)(2,1)S(1)} %fusion.1087), channel_id=1, source_target_pairs={{1,0},{2,1},{3,2},{4,3},{5,4},{6,5},{7,6}} | collective-permute-start | bytes 1966088 | tf_op jit(solution)/shard_map/ppermute | solution.py:57
  1016.5 12.8 %collective-permute-start.37 = (bf16[512,640]{1,0:T(8,128)(2,1)S(1)}, bf16[512,640]{1,0:T(8,128)(2,1)S(1)}, u32[]{:S(2)}, u32[]{:S(2)}) collective-permute-start(bf16[512,640]{1,0:T(8,128)(2,1)S(1)} %fusion.1084), channel_id=1, source_target_pairs={{1,0},{2,1},{3,2},{4,3},{5,4},{6,5},{7,6}} | collective-permute-start | bytes 1966088 | tf_op jit(solution)/shard_map/ppermute | solution.py:57
  (154 other events, 1190.9 us)
where the time goes:
time: 1270 us; the launch traced here: 1260 us
  matrix products  714 us (56%)
  waiting for transfers between devices  243 us (19%)
  starting transfers between devices  166 us (13%)
  other arithmetic  79.8 us (6%)
  local copies, waits for them, and re-layouts  56.7 us (4%)
    dot_general x68, matrix products, matmul(): jnp.dot(a, w, preferred_element_type=jnp.float32).astype(jnp.bfloat16)  276 us
    dot_general x90, matrix products, layer(): gate = jnp.dot(a, w['w_gate'], preferred_element_type=jnp.float32)  242 us
    dot_general x68, matrix products, layer(): up = jnp.dot(a, w['w_up'], preferred_element_type=jnp.float32)  197 us
    ppermute x22, waiting for transfers between devices, step(): came = lax.ppermute(by_h, 'pp', back_again)  156 us
    ppermute x22, starting transfers between devices, step(): came = lax.ppermute(stage(weights, h), 'pp', onward)  118 us
    ppermute x22, waiting for transfers between devices, step(): came = lax.ppermute(stage(weights, h), 'pp', onward)  86 us
    ppermute x22, starting transfers between devices, step(): came = lax.ppermute(by_h, 'pp', back_again)  47.6 us
    dynamic_update_slice x23, other arithmetic, step(): lax.dynamic_update_index_in_dim(kept, jnp.where(at_work, h, was), number, 0)  35.6 us
  transfers between devices with their start and end apart: 44, of which 40 were waited for; matrix products, arithmetic and copies ran while one was open for 15% of the time, Pallas kernels for 0%

commit v1 on v0

v1 whole, which is shorter than its diff:
```python
import functools

import jax
import jax.numpy as jnp
from jax import lax
from jax.experimental import pallas as pl
from jax.experimental.pallas import tpu as pltpu
from jax.sharding import PartitionSpec as P

BF, F32 = jnp.bfloat16, jnp.float32
MESH = pl.DeviceIdType.MESH
NN = (((1,), (0,)), ((), ()))
NT = (((1,), (1,)), ((), ()))
TN = (((0,), (0,)), ((), ()))
BLOCK = 256
WIDTH = 256
T = 256


def dot(a, b, dims=NN):
    return lax.dot_general(a, b, dims, preferred_element_type=F32)


def scale_of(wide):
    return lax.rsqrt(jnp.mean(wide * wide, 0, keepdims=True) + 1e-6)


def kernel(stages, x, dy, wg_in, wu_in, wd_in, wg_out, wu_out, wd_out, gu_hbm,
           wg, wu, wd, tg, tu, td, h, dh, gu, dg, du, pb, ab, pf, y_out, dh_out, fresh,
           w_sem, x_sem, gu_put, gu_get, y_send, y_recv, dh_send, dh_recv):
    me = lax.axis_index("pp")
    last = stages - 1
    micro, tokens, d = x.shape
    ff = wg.shape[1]
    per = tokens // T
    chunks = micro * per
    right, left = lax.rem(me + 1, stages), lax.rem(me + stages - 1, stages)
    ahead = per * (last - me)
    spill = ahead > 3

    def chunk_of(array, c):
        return array.at[c // per, pl.ds(pl.multiple_of(c % per * T, T), T), :]

    def load(array, c):
        return pltpu.make_async_copy(chunk_of(array, c), fresh.at[c % 2], x_sem.at[c % 2])

    def send_y(c):
        return pltpu.make_async_remote_copy(
            src_ref=y_out.at[c % 2], dst_ref=h.at[c], send_sem=y_send.at[c % 2], recv_sem=y_recv.at[c],
            device_id={"pp": right}, device_id_type=MESH)

    def send_dh(c):
        return pltpu.make_async_remote_copy(
            src_ref=dh_out.at[c % 2], dst_ref=dh.at[c], send_sem=dh_send.at[c % 2], recv_sem=dh_recv.at[c],
            device_id={"pp": left}, device_id_type=MESH)

    def put_gu(c):
        return pltpu.make_async_copy(gu.at[c % 2], gu_hbm.at[c], gu_put.at[c % 2])

    def get_gu(c):
        return pltpu.make_async_copy(gu_hbm.at[c], gu.at[2 + c % 2], gu_get.at[c % 2])

    barrier = pltpu.get_barrier_semaphore()

    @pl.when(me > 0)
    def _():
        pl.semaphore_signal(barrier, inc=1, device_id={"pp": left}, device_id_type=MESH)

    @pl.when(me < last)
    def _():
        pl.semaphore_signal(barrier, inc=1, device_id={"pp": right}, device_id_type=MESH)

    w_copies = [pltpu.make_async_copy(s, t, w_sem.at[i]) for i, (s, t) in enumerate(((wg_in, wg), (wu_in, wu), (wd_in, wd)))]
    @pl.when(me == 0)
    def _():
        load(x, 0).start()
        load(x, 1).start()

    for copy in w_copies:
        copy.start()

    def clear():
        for total in (tg, tu, td):
            total[...] = jnp.zeros_like(total)

    @pl.when(me == last)
    def _():
        load(dy, 0).start()
        load(dy, 1).start()

        def turn(c, _):
            load(dy, c).wait()
            dh[c] = fresh[c % 2].T

            @pl.when(c + 2 < chunks)
            def _():
                load(dy, c + 2).start()

            return 0

        lax.fori_loop(0, chunks, turn, 0)

    @pl.when(me > 0)
    def _():
        clear()

    for copy in w_copies:
        copy.wait()

    pl.semaphore_wait(barrier, jnp.where((me > 0) & (me < last), 2, 1))

    def up_and_gate(c, down):
        slot = jnp.where(spill, c % 2, c % 4)
        wide = h[c].astype(F32)
        a = (wide * scale_of(wide)).astype(BF)
        for j in range(ff // BLOCK):
            here = pl.ds(j * BLOCK, BLOCK)
            gate, up = dot(wg[:, here], a, TN), dot(wu[:, here], a, TN)
            gu[slot, here, :] = gate
            gu[slot, pl.ds(ff + j * BLOCK, BLOCK), :] = up
            if down:
                pf[here, :] = (gate * jax.nn.sigmoid(gate) * up).astype(BF)
        if down:
            y_out[c % 2] = h[c] + dot(wd[...], pf[...], TN).astype(BF)

    def forward(c):
        @pl.when(me == 0)
        def _():
            load(x, c).wait()
            h[c] = fresh[c % 2].T

            @pl.when(c + 2 < chunks)
            def _():
                load(x, c + 2).start()

        @pl.when(me > 0)
        def _():
            send_y(c).wait_recv()

        @pl.when(me < last)
        def _():
            @pl.when(c >= 2)
            def _():
                send_y(c - 2).wait_send()

            up_and_gate(c, True)
            send_y(c).start()

        @pl.when(me == last)
        def _():
            up_and_gate(c, False)

        @pl.when(spill)
        def _():
            put_gu(c).start()

    def hidden_back(c):
        slot = jnp.where(spill, 2 + c % 2, c % 4)
        half = c % per
        by_y = dh[c]
        for j in range(ff // BLOCK):
            here = pl.ds(j * BLOCK, BLOCK)
            by_p = dot(wd[here, :], by_y).astype(BF).astype(F32)
            gate, up = gu[slot, here, :], gu[slot, pl.ds(ff + j * BLOCK, BLOCK), :]
            sig = jax.nn.sigmoid(gate)
            silu = gate * sig
            pb[half, here, :] = (silu * up).astype(BF)
            du[half, here, :] = (silu * by_p).astype(BF)
            dg[half, here, :] = (up * by_p * (sig + silu * (1 - sig))).astype(BF)

    def state_back(c):
        half = c % per
        wide = h[c].astype(F32)
        scale = scale_of(wide)
        ab[half] = (wide * scale).astype(BF)
        by_a = (dot(wg[...], dg[half]).astype(BF) + dot(wu[...], du[half]).astype(BF)).astype(F32)
        along = jnp.sum(by_a * wide, 0, keepdims=True) * (scale * scale * scale) * (1.0 / d)
        dh_out[c % 2] = dh[c] + (by_a * scale - wide * along).astype(BF)

    def backward(c):
        @pl.when(me < last)
        def _():
            send_dh(c).wait_recv()

        @pl.when(me > 0)
        def _():
            @pl.when(c >= 2)
            def _():
                send_dh(c - 2).wait_send()

            hidden_back(c)
            state_back(c)
            send_dh(c).start()

        @pl.when(me == 0)
        def _():
            hidden_back(c)
            wide = h[c].astype(F32)
            ab[c % per] = (wide * scale_of(wide)).astype(BF)

    def weights_back(m):
        first = m * per
        for j in range(ff // WIDTH):
            here = pl.ds(j * WIDTH, WIDTH)
            for lhs, at, rhs, total in ((ab, 0, dg, tg), (ab, 0, du, tu), (dh, first, pb, td)):
                term = sum(dot(lhs[at + i], rhs[i, here, :], NT) for i in range(per))
                total[:, here] += term.astype(BF).astype(F32)

    def step(t, _):
        c = t - ahead

        @pl.when(spill & (t >= 2) & (t < chunks + 2))
        def _():
            put_gu(t - 2).wait()

        @pl.when(spill & (c + 1 >= 0) & (c + 1 < chunks))
        def _():
            get_gu(c + 1).start()

        @pl.when(t < chunks)
        def _():
            forward(t)

        @pl.when((me == 0) & (t == 2))
        def _():
            clear()

        @pl.when(c >= 0)
        def _():
            @pl.when(spill)
            def _():
                get_gu(c).wait()

            backward(c)

            @pl.when(c % per == per - 1)
            def _():
                weights_back(c // per)

        return 0

    lax.fori_loop(0, chunks + ahead, step, 0)

    wg[...] = tg[...].astype(BF)
    out_g = pltpu.make_async_copy(wg, wg_out, w_sem.at[0])
    out_g.start()
    wu[...] = tu[...].astype(BF)
    out_u = pltpu.make_async_copy(wu, wu_out, w_sem.at[1])
    out_u.start()
    wd[...] = td[...].astype(BF).T
    out_d = pltpu.make_async_copy(wd, wd_out, w_sem.at[2])
    out_d.start()
    for copy in (out_g, out_u, out_d):
        copy.wait()

    @pl.when(me < last)
    def _():
        for c in (chunks - 2, chunks - 1):
            send_y(c).wait_send()

    @pl.when(me > 0)
    def _():
        for c in (chunks - 2, chunks - 1):
            send_dh(c).wait_send()


def solution(mesh):
    stages = mesh.shape["pp"]

    def step(x, dy, wg, wu, wd):
        micro, tokens, d = x.shape
        ff = wg.shape[2]
        per = tokens // T
        chunks = micro * per
        vmem, dma = pltpu.VMEM, pltpu.SemaphoreType.DMA
        hbm = pl.BlockSpec(memory_space=pl.ANY)
        outs = pl.pallas_call(
            functools.partial(kernel, stages),
            out_shape=(
                jax.ShapeDtypeStruct((d, ff), BF),
                jax.ShapeDtypeStruct((d, ff), BF),
                jax.ShapeDtypeStruct((ff, d), BF),
                jax.ShapeDtypeStruct((chunks, 2 * ff, T), F32),
            ),
            in_specs=[hbm] * 5,
            out_specs=[hbm] * 4,
            scratch_shapes=[
                vmem((d, ff), BF), vmem((d, ff), BF), vmem((ff, d), BF),
                vmem((d, ff), F32), vmem((d, ff), F32), vmem((d, ff), F32),
                vmem((chunks, d, T), BF), vmem((chunks, d, T), BF),
                vmem((4, 2 * ff, T), F32),
                vmem((per, ff, T), BF), vmem((per, ff, T), BF), vmem((per, ff, T), BF),
                vmem((per, d, T), BF), vmem((ff, T), BF),
                vmem((2, d, T), BF), vmem((2, d, T), BF), vmem((2, T, d), BF),
                dma((3,)), dma((2,)), dma((2,)), dma((2,)), dma((2,)), dma((chunks,)), dma((2,)), dma((chunks,)),
            ],
            compiler_params=pltpu.CompilerParams(collective_id=0, has_side_effects=True, vmem_limit_bytes=67043328),
        )(x, dy, wg[0], wu[0], wd[0])
        return tuple(o[None] for o in outs[:3])

    return jax.shard_map(
        step,
        mesh=mesh,
        in_specs=(P("rep", None, None),) * 2 + (P("pp", None, None),) * 3,
        out_specs=(P(("rep", "pp"), None, None),) * 3,
        check_vma=False,
    )
```

time: 1270 us -> 350 us (0.28)
  the two profiles are of different devices: /device:TPU:5 before, /device:TPU:0 now
where the time goes in v1:
time: 350 us; the launch traced here: 349 us
  Pallas kernels  342 us (98%)
  local copies, waits for them, and re-layouts  6.61 us (2%)
    pallas_call x1, Pallas kernels, step(): pl.pallas_call(functools.partial(kernel, stages), out_shape=(jax.ShapeDty...  342 us

profile of v1, /device:TPU:0, one launch (start us, length us, event | category | flops | bytes accessed | tf_op | source)
XLA Modules:
  0.0 349.4 jit_solution(11660836226119752249)
XLA Ops:
  0.6 342.1 %shard_map.76 = (bf16[640,1536]{1,0:T(8,128)(2,1)}, bf16[640,1536]{1,0:T(8,128)(2,1)}, bf16[1536,640]{1,0:T(8,128)(2,1)}, f32[32,3072,256]{2,1,0:T(8,128)}) custom-call(bf16[16,512,640]{2,1,0:T(8,128)(2,1)} %x.1, bf16[16,512,640]{2,1,0:T(8,128)(2,1)} %dy.1, bf16[640,1536]{1,0:T(8,128)(2,1)} %bitcast.6, bf16[640,1536]{1,0:T(8,128)(2,1)} %bitcast.7, ...), custom_call_target="tpu_custom_call" | custom-call | tf_op jit(solution)/shard_map/pallas_call | solution.py:277
  342.8 0.0 copy-start.1
  342.8 3.1 copy.11
  345.9 0.0 copy-done.1
  345.9 0.0 copy-start
  345.9 1.3 copy.12
  347.1 1.0 copy-done
  348.1 1.3 copy.13
Async XLA Ops:
  342.8 3.1 copy-start.1
  345.9 2.3 copy-start

commit v2 on v1

v2 whole, which is shorter than its diff:
```python
import functools

import jax
import jax.numpy as jnp
from jax import lax
from jax.experimental import pallas as pl
from jax.experimental.pallas import tpu as pltpu
from jax.sharding import PartitionSpec as P

BF, F32 = jnp.bfloat16, jnp.float32
MESH = pl.DeviceIdType.MESH
NN = (((1,), (0,)), ((), ()))
NT = (((1,), (1,)), ((), ()))
TN = (((0,), (0,)), ((), ()))
FORTH, BACK = 256, 512
WIDTH = 256
T = 256
RING = 2
DIGITS = 10
ORDER = (
    (153391689, 153391689, 203821641, 176507172, 476398235, 458307794, 461977250, 325662370, 441296090, 325662355, 441296090, 3),
    (153391689, 153391689, 321720969, 172339849, 304980635, 323597467, 309143251, 457815195, 309143250, 111771),
    (153391689, 170168905, 423958218, 455647827, 292099786, 458036875, 309143250, 457815195, 309143250, 111771),
    (153391689, 438866505, 325362889, 442807433, 438871115, 438940299, 457778899, 443131546, 443131546, 111834),
    (170168905, 155493978, 321492170, 174404249, 174892627, 170435227, 170435227, 306783378, 460175067, 112347),
    (289706569, 439161947, 189576273, 292074698, 291837521, 455648970, 170435210, 306783370, 460175067, 112347),
    (291837001, 292135626, 439161499, 290300555, 170202187, 289972874, 289739857, 460137553, 460175067, 112347),
    (289780817, 191960155, 171029588, 474290394, 292430475, 170440332, 289809034, 289741073, 289739857, 460175067, 898843),
)


LATER = (16, 16, 16, 16, 8, 8, 6, 8)


ON, BY_ON = 0, (8, 9, 10, 11, 12, 14, 16, 18, 20, 22, 23, 25, 28, 30, 31)
OFF, BY_OFF = 7, (0, 1, 2, 4, 5, 7, 8, 13, 15, 16, 31)


def among(c, chosen):
    return sum([jnp.where(c == k, 1, 0) for k in chosen], jnp.int32(0)) > 0


def place(c, chosen):
    return sum([jnp.where(c == k, i, 0) for i, k in enumerate(chosen)], jnp.int32(0))


def nth(r, chosen):
    return sum([jnp.where(r == i, k, 0) for i, k in enumerate(chosen)], jnp.int32(0))


def dot(a, b, dims=NN):
    return lax.dot_general(a, b, dims, preferred_element_type=F32)


def scale_of(wide):
    return lax.rsqrt(jnp.mean(wide * wide, 0, keepdims=True) + 1e-6)


def kernel(stages, x, dy, wg_in, wu_in, wd_in, wg_out, wu_out, wd_out, gu_hbm, post, kept,
           wg, wu, wd, tg, tu, td, h, dh, gu, terms, pf, y_out, dh_out, fresh,
           w_sem, x_sem, gu_put, gu_get, y_send, y_recv, dh_send, dh_recv, post_recv, post_send, keep, fetch):
    me = lax.axis_index("pp")
    last = stages - 1
    micro, tokens, d = x.shape
    ff = wg.shape[1]
    per = tokens // T
    chunks = micro * per
    right, left = lax.rem(me + 1, stages), lax.rem(me + stages - 1, stages)
    spill = me < last - 1
    pairs = [(i, i + 1) for i in range(last)] + [(0, 3), (0, 4), (3, 7), (4, 7)]

    later = sum(jnp.where(me == s, number, 0) for s, number in enumerate(LATER))

    def chunk_of(array, c):
        return array.at[c >> 1, pl.ds(pl.multiple_of((c & 1) * T, T), T), :]

    def load(array, c):
        return pltpu.make_async_copy(chunk_of(array, c), fresh.at[c & 1], x_sem.at[c & 1])

    def send_y(c):
        return pltpu.make_async_remote_copy(
            src_ref=y_out.at[c & 1], dst_ref=h.at[c], send_sem=y_send.at[c & 1], recv_sem=y_recv.at[c],
            device_id={"pp": right}, device_id_type=MESH)

    def send_dh(c):
        return pltpu.make_async_remote_copy(
            src_ref=dh_out.at[c & 1], dst_ref=dh.at[c], send_sem=dh_send.at[c & 1], recv_sem=dh_recv.at[c],
            device_id={"pp": left}, device_id_type=MESH)

    def post_to(source, c, r, target):
        return pltpu.make_async_remote_copy(
            src_ref=source.at[c & 1], dst_ref=post.at[r], send_sem=(y_send if target == 0 else dh_send).at[c & 1],
            recv_sem=post_recv.at[r], device_id={"pp": target}, device_id_type=MESH)

    def post_on(r):
        return pltpu.make_async_remote_copy(
            src_ref=post.at[r], dst_ref=h.at[nth(r, BY_ON)], send_sem=post_send.at[r], recv_sem=y_recv.at[nth(r, BY_ON)],
            device_id={"pp": 4}, device_id_type=MESH)

    def post_back(r):
        return pltpu.make_async_remote_copy(
            src_ref=post.at[r], dst_ref=dh.at[nth(r, BY_OFF)], send_sem=post_send.at[r], recv_sem=dh_recv.at[nth(r, BY_OFF)],
            device_id={"pp": 3}, device_id_type=MESH)

    def keep_terms(m):
        return pltpu.make_async_copy(terms.at[m & 1], kept.at[m], keep.at[m & 1])

    def fetch_terms(m):
        return pltpu.make_async_copy(kept.at[m], terms.at[m & 1], fetch.at[m & 1])

    def put_gu(c):
        return pltpu.make_async_copy(gu.at[c & 1], gu_hbm.at[c], gu_put.at[c & 1])

    def get_gu(c):
        return pltpu.make_async_copy(gu_hbm.at[c], gu.at[2 + (c & 1)], gu_get.at[c & 1])

    barrier = pltpu.get_barrier_semaphore()

    for one, two in pairs:
        for here, there in ((one, two), (two, one)):
            @pl.when(me == here)
            def _():
                pl.semaphore_signal(barrier, inc=1, device_id={"pp": there}, device_id_type=MESH)

    w_copies = [pltpu.make_async_copy(s, t, w_sem.at[i]) for i, (s, t) in enumerate(((wg_in, wg), (wu_in, wu), (wd_in, wd)))]
    @pl.when(me == 0)
    def _():
        load(x, 0).start()
        load(x, 1).start()

    for copy in w_copies:
        copy.start()

    def clear():
        for total in (tg, tu, td):
            total[...] = jnp.zeros_like(total)

    @pl.when(me == last)
    def _():
        load(dy, 0).start()
        load(dy, 1).start()

        def turn(c, _):
            load(dy, c).wait()
            dh[c] = fresh[c & 1].T

            @pl.when(c + 2 < chunks)
            def _():
                load(dy, c + 2).start()

            return 0

        lax.fori_loop(0, chunks, turn, 0)

    @pl.when(me > 0)
    def _():
        clear()

    for copy in w_copies:
        copy.wait()

    pl.semaphore_wait(barrier, sum(jnp.where((me == one) | (me == two), 1, 0) for one, two in pairs))

    def up_and_gate(c, down):
        slot = jnp.where(spill, c & 1, c & 3)
        wide = h[c].astype(F32)
        a = (wide * scale_of(wide)).astype(BF)
        for j in range(ff // FORTH):
            here = pl.ds(j * FORTH, FORTH)
            gate, up = dot(wg[:, here], a, TN), dot(wu[:, here], a, TN)
            gu[slot, here, :] = gate
            gu[slot, pl.ds(ff + j * FORTH, FORTH), :] = up
            if down:
                pf[here, :] = (gate * jax.nn.sigmoid(gate) * up).astype(BF)
        if down:
            y_out[c & 1] = h[c] + dot(wd[...], pf[...], TN).astype(BF)

    def forward(c, put):
        @pl.when(spill & (c >= 2) & (put == c - 2))
        def _():
            put_gu(c - 2).wait()

        @pl.when(me == 0)
        def _():
            load(x, c).wait()
            h[c] = fresh[c & 1].T

            @pl.when(c + 2 < chunks)
            def _():
                load(x, c + 2).start()

        @pl.when(me > 0)
        def _():
            send_y(c).wait_recv()

        @pl.when(me < last)
        def _():
            @pl.when(c >= 2)
            def _():
                send_y(c - 2).wait_send()

            up_and_gate(c, True)

        @pl.when((me < last) & ~((me == 3) & among(c, BY_ON)))
        def _():
            send_y(c).start()

        @pl.when((me == 3) & among(c, BY_ON))
        def _():
            post_to(y_out, c, place(c, BY_ON), 0).start()

        @pl.when(me == last)
        def _():
            up_and_gate(c, False)

        @pl.when(spill)
        def _():
            put_gu(c).start()

        @pl.when(spill & (c == 2))
        def _():
            get_gu(0).start()

    def hidden_back(c):
        slot = jnp.where(spill, 2 + (c & 1), c & 3)
        at, half = (c >> 1) & 1, c & 1
        by_y = dh[c]
        for j in range(ff // BACK):
            here = pl.ds(j * BACK, BACK)
            by_p = dot(wd[here, :], by_y).astype(BF).astype(F32)
            gate, up = gu[slot, here, :], gu[slot, pl.ds(ff + j * BACK, BACK), :]
            sig = jax.nn.sigmoid(gate)
            silu = gate * sig
            terms[at, 2, half, here, :] = (silu * up).astype(BF)
            terms[at, 1, half, here, :] = (silu * by_p).astype(BF)
            terms[at, 0, half, here, :] = (up * by_p * (sig + silu * (1 - sig))).astype(BF)

    def state_back(c):
        at, half = (c >> 1) & 1, c & 1
        wide = h[c].astype(F32)
        scale = scale_of(wide)
        by_a = (dot(wg[...], terms[at, 0, half]).astype(BF) + dot(wu[...], terms[at, 1, half]).astype(BF)).astype(F32)
        along = jnp.sum(by_a * wide, 0, keepdims=True) * (scale * scale * scale) * (1.0 / d)
        dh_out[c & 1] = dh[c] + (by_a * scale - wide * along).astype(BF)
        h[c] = (wide * scale).astype(BF)

    def backward(c, put):
        for k in (c, c + 1):
            @pl.when(spill & (put <= k) & (k < chunks))
            def _():
                put_gu(k).wait()

        @pl.when(((c & 1) == 0) & ((c >> 1) >= later + 2))
        def _():
            keep_terms((c >> 1) - 2).wait()

        @pl.when(spill & (c + 1 < chunks))
        def _():
            get_gu(c + 1).start()

        @pl.when(spill)
        def _():
            get_gu(c).wait()

        @pl.when(me < last)
        def _():
            send_dh(c).wait_recv()

        @pl.when(me > 0)
        def _():
            @pl.when(c >= 2)
            def _():
                send_dh(c - 2).wait_send()

            hidden_back(c)
            state_back(c)

        @pl.when((me > 0) & ~((me == 4) & among(c, BY_OFF)))
        def _():
            send_dh(c).start()

        @pl.when((me == 4) & among(c, BY_OFF))
        def _():
            post_to(dh_out, c, place(c, BY_OFF), 7).start()

        @pl.when(((c & 1) == 1) & ((c >> 1) >= later))
        def _():
            keep_terms(c >> 1).start()

        @pl.when((c == chunks - 1) & (later < micro))
        def _():
            keep_terms(micro - 2).wait()
            fetch_terms(later).start()

        @pl.when(me == 0)
        def _():
            hidden_back(c)
            wide = h[c].astype(F32)
            h[c] = (wide * scale_of(wide)).astype(BF)

    def weights_back(n):
        m, half = n >> 1, n & 1

        @pl.when((half == 0) & (m >= later))
        def _():
            @pl.when(m == later)
            def _():
                keep_terms(micro - 1).wait()
                fetch_terms(later + 1).start()

            fetch_terms(m).wait()

        for j in range(ff // 2 // WIDTH):
            here = pl.ds(pl.multiple_of(half * (ff // 2) + j * WIDTH, WIDTH), WIDTH)
            for lhs, i, total in ((h, 0, tg), (h, 1, tu), (dh, 2, td)):
                term = sum(dot(lhs[m * per + k], terms[m & 1, i, k, here, :], NT) for k in range(per))
                total[:, here] += term.astype(BF).astype(F32)

        @pl.when((half == 1) & (m >= later) & (m + 2 < micro))
        def _():
            fetch_terms(m + 2).start()

    def hand_on(r):
        pltpu.make_async_remote_copy(
            src_ref=y_out.at[0], dst_ref=post.at[r], send_sem=y_send.at[0], recv_sem=post_recv.at[r],
            device_id={"pp": right}, device_id_type=MESH).wait_recv()

        @pl.when(me == 0)
        def _():
            post_on(r).start()

        @pl.when(me == last)
        def _():
            post_back(r).start()

    def word(q, carry):
        code = sum(jnp.where((me == s) & (q == i), number, 0) for s, row in enumerate(ORDER) for i, number in enumerate(row) if number)

        def operation(_, carry):
            code, on, back, done, handed, put = carry
            kind = code & 7

            @pl.when(kind == 1)
            def _():
                forward(on, put)

            @pl.when((kind == 1) & (me == 0) & (on == 2))
            def _():
                clear()

            @pl.when(kind == 2)
            def _():
                backward(back, put)

            @pl.when(kind == 3)
            def _():
                weights_back(done)

            @pl.when(kind == 4)
            def _():
                hand_on(handed)

            put = jnp.where(kind == 1, jnp.maximum(put, on - 1), put)
            put = jnp.where(kind == 2, jnp.maximum(put, jnp.minimum(back + 2, chunks)), put)
            one = [jnp.where(kind == k, 1, 0) for k in (1, 2, 3, 4)]
            return code >> 3, on + one[0], back + one[1], done + one[2], handed + one[3], put

        return lax.fori_loop(0, DIGITS, operation, (code, *carry))[1:]

    lax.fori_loop(0, max(len(row) for row in ORDER), word, (jnp.int32(0),) * 5)

    wg[...] = tg[...].astype(BF)
    out_g = pltpu.make_async_copy(wg, wg_out, w_sem.at[0])
    out_g.start()
    wu[...] = tu[...].astype(BF)
    out_u = pltpu.make_async_copy(wu, wu_out, w_sem.at[1])
    out_u.start()
    wd[...] = td[...].astype(BF).T
    out_d = pltpu.make_async_copy(wd, wd_out, w_sem.at[2])
    out_d.start()
    for copy in (out_g, out_u, out_d):
        copy.wait()

    @pl.when(me < last)
    def _():
        for c in (chunks - 2, chunks - 1):
            send_y(c).wait_send()

    @pl.when(me > 0)
    def _():
        for c in (chunks - 2, chunks - 1):
            send_dh(c).wait_send()

    def sent(r, _):
        post_on(r).wait_send()
        return 0

    lax.fori_loop(0, jnp.where(me == 0, len(BY_ON), jnp.where(me == last, len(BY_OFF), 0)), sent, 0)


def solution(mesh):
    stages = mesh.shape["pp"]

    def step(x, dy, wg, wu, wd):
        micro, tokens, d = x.shape
        ff = wg.shape[2]
        per = tokens // T
        chunks = micro * per
        vmem, dma = pltpu.VMEM, pltpu.SemaphoreType.DMA
        hbm = pl.BlockSpec(memory_space=pl.ANY)
        outs = pl.pallas_call(
            functools.partial(kernel, stages),
            out_shape=(
                jax.ShapeDtypeStruct((d, ff), BF),
                jax.ShapeDtypeStruct((d, ff), BF),
                jax.ShapeDtypeStruct((ff, d), BF),
                jax.ShapeDtypeStruct((chunks, 2 * ff, T), F32),
                jax.ShapeDtypeStruct((16, d, T), BF),
                jax.ShapeDtypeStruct((micro, 3, per, ff, T), BF),
            ),
            in_specs=[hbm] * 5,
            out_specs=[hbm] * 6,
            scratch_shapes=[
                vmem((d, ff), BF), vmem((d, ff), BF), vmem((ff, d), BF),
                vmem((d, ff), F32), vmem((d, ff), F32), vmem((d, ff), F32),
                vmem((chunks, d, T), BF), vmem((chunks, d, T), BF),
                vmem((4, 2 * ff, T), F32),
                vmem((RING, 3, per, ff, T), BF), vmem((ff, T), BF),
                vmem((2, d, T), BF), vmem((2, d, T), BF), vmem((2, T, d), BF),
                dma((3,)), dma((2,)), dma((2,)), dma((2,)), dma((2,)), dma((chunks,)), dma((2,)), dma((chunks,)), dma((16,)), dma((16,)), dma((2,)), dma((2,)),
            ],
            compiler_params=pltpu.CompilerParams(collective_id=0, has_side_effects=True, vmem_limit_bytes=67043328),
        )(x, dy, wg[0], wu[0], wd[0])
        return tuple(o[None] for o in outs[:3])

    return jax.shard_map(
        step,
        mesh=mesh,
        in_specs=(P("rep", None, None),) * 2 + (P("pp", None, None),) * 3,
        out_specs=(P(("rep", "pp"), None, None),) * 3,
        check_vma=False,
    )
```

time: 350 us -> 287 us (0.82)
  Pallas kernels: 342 us -> 279 us
    pallas_call x1, Pallas kernels: 342 us -> 279 us  [step(): pl.pallas_call(functools.partial(kernel, stages), out_shape=(jax.ShapeDty...]
where the time goes in v2:
time: 287 us
  Pallas kernels  279 us (97%)
  local copies, waits for them, and re-layouts  6.61 us (2%)
    pallas_call x1, Pallas kernels, step(): pl.pallas_call(functools.partial(kernel, stages), out_shape=(jax.ShapeDty...  279 us
    unnamed x7, local copies, waits for them, and re-layouts  6.61 us

profile of v2, /device:TPU:0, one launch (start us, length us, event | category | flops | bytes accessed | tf_op | source)
XLA Modules:
  0.0 286.7 jit_solution(12630885521999973778)
XLA Ops:
  0.6 279.4 %shard_map.76 = (bf16[640,1536]{1,0:T(8,128)(2,1)}, bf16[640,1536]{1,0:T(8,128)(2,1)}, bf16[1536,640]{1,0:T(8,128)(2,1)}, f32[32,3072,256]{2,1,0:T(8,128)}, bf16...) custom-call(bf16[16,512,640]{2,1,0:T(8,128)(2,1)} %x.1, bf16[16,512,640]{2,1,0:T(8,128)(2,1)} %dy.1, ...), custom_call_target="tpu_custom_call" | custom-call | tf_op jit(solution)/shard_map/pallas_call | solution.py:411
  280.0 0.0 copy-start.1
  280.1 3.1 %copy.11 = bf16[1,640,1536]{2,1,0:T(8,128)(2,1)} copy(bf16[1,640,1536]{2,1,0:T(8,128)(2,1)} %bitcast.11) | data formatting | bytes 3932160
  283.1 0.0 copy-done.1
  283.1 0.0 copy-start
  283.1 1.3 copy.12
  284.4 1.0 copy-done
  285.4 1.3 copy.13
Async XLA Ops:
  280.0 3.1 %copy-start.1 = (bf16[640,1536]{1,0:T(8,128)(2,1)S(1)}, bf16[640,1536]{1,0:T(8,128)(2,1)}, u32[]{:S(2)}) copy-start(bf16[640,1536]{1,0:T(8,128)(2,1)} %get-tuple-element.7) | copy-start | bytes 5898244
  283.1 2.3 copy-start

commit v3 on v2

--- a/solution.py
+++ b/solution.py
@@ -175,7 +175,7 @@
         if down:
             y_out[c & 1] = h[c] + dot(wd[...], pf[...], TN).astype(BF)
 
-    def forward(c, put):
+    def before_forward(c, put):
         @pl.when(spill & (c >= 2) & (put == c - 2))
         def _():
             put_gu(c - 2).wait()
@@ -193,33 +193,47 @@
         def _():
             send_y(c).wait_recv()
 
+        @pl.when((me < last) & (c >= 2))
+        def _():
+            send_y(c - 2).wait_send()
+
+    def after_forward(c):
+        @pl.when(spill)
+        def _():
+            put_gu(c).start()
+
+            @pl.when(c == 2)
+            def _():
+                get_gu(0).start()
+
+    def forward(c, put):
+        before_forward(c, put)
+
         @pl.when(me < last)
         def _():
-            @pl.when(c >= 2)
-            def _():
-                send_y(c - 2).wait_send()
-
             up_and_gate(c, True)
 
-        @pl.when((me < last) & ~((me == 3) & among(c, BY_ON)))
-        def _():
-            send_y(c).start()
-
-        @pl.when((me == 3) & among(c, BY_ON))
-        def _():
-            post_to(y_out, c, place(c, BY_ON), 0).start()
+            @pl.when(me != 3)
+            def _():
+                send_y(c).start()
+
+            @pl.when(me == 3)
+            def _():
+                relayed = among(c, BY_ON)
+
+                @pl.when(~relayed)
+                def _():
+                    send_y(c).start()
+
+                @pl.when(relayed)
+                def _():
+                    post_to(y_out, c, place(c, BY_ON), 0).start()
 
         @pl.when(me == last)
         def _():
             up_and_gate(c, False)
 
-        @pl.when(spill)
-        def _():
-            put_gu(c).start()
-
-        @pl.when(spill & (c == 2))
-        def _():
-            get_gu(0).start()
+        after_forward(c)
 
     def hidden_back(c):
         slot = jnp.where(spill, 2 + (c & 1), c & 3)
@@ -244,53 +258,65 @@
         dh_out[c & 1] = dh[c] + (by_a * scale - wide * along).astype(BF)
         h[c] = (wide * scale).astype(BF)
 
+    def before_backward(c, put):
+        @pl.when(((c & 1) == 0) & ((c >> 1) >= later + 2))
+        def _():
+            keep_terms((c >> 1) - 2).wait()
+
+        @pl.when(spill)
+        def _():
+            for k in (c, c + 1):
+                @pl.when((put <= k) & (k < chunks))
+                def _():
+                    put_gu(k).wait()
+
+            @pl.when(c + 1 < chunks)
+            def _():
+                get_gu(c + 1).start()
+
+            get_gu(c).wait()
+
+        @pl.when(me < last)
+        def _():
+            send_dh(c).wait_recv()
+
+        @pl.when((me > 0) & (c >= 2))
+        def _():
+            send_dh(c - 2).wait_send()
+
+    def after_backward(c):
+        @pl.when(((c & 1) == 1) & ((c >> 1) >= later))
+        def _():
+            keep_terms(c >> 1).start()
+
+            @pl.when(c == chunks - 1)
+            def _():
+                keep_terms(micro - 2).wait()
+                fetch_terms(later).start()
+
     def backward(c, put):
-        for k in (c, c + 1):
-            @pl.when(spill & (put <= k) & (k < chunks))
-            def _():
-                put_gu(k).wait()
-
-        @pl.when(((c & 1) == 0) & ((c >> 1) >= later + 2))
-        def _():
-            keep_terms((c >> 1) - 2).wait()
-
-        @pl.when(spill & (c + 1 < chunks))
-        def _():
-            get_gu(c + 1).start()
-
-        @pl.when(spill)
-        def _():
-            get_gu(c).wait()
-
-        @pl.when(me < last)
-        def _():
-            send_dh(c).wait_recv()
+        before_backward(c, put)
 
         @pl.when(me > 0)
         def _():
-            @pl.when(c >= 2)
-            def _():
-                send_dh(c - 2).wait_send()
-
             hidden_back(c)
             state_back(c)
 
-        @pl.when((me > 0) & ~((me == 4) & among(c, BY_OFF)))
-        def _():
-            send_dh(c).start()
-
-        @pl.when((me == 4) & among(c, BY_OFF))
-        def _():
-            post_to(dh_out, c, place(c, BY_OFF), 7).start()
-
-        @pl.when(((c & 1) == 1) & ((c >> 1) >= later))
-        def _():
-            keep_terms(c >> 1).start()
-
-        @pl.when((c == chunks - 1) & (later < micro))
-        def _():
-            keep_terms(micro - 2).wait()
-            fetch_terms(later).start()
+            @pl.when(me != 4)
+            def _():
+                send_dh(c).start()
+
+            @pl.when(me == 4)
+            def _():
+                relayed = among(c, BY_OFF)
+
+                @pl.when(~relayed)
+                def _():
+                    send_dh(c).start()
+
+                @pl.when(relayed)
+                def _():
+                    post_to(dh_out, c, place(c, BY_OFF), 7).start()
 
         @pl.when(me == 0)
         def _():
@@ -298,6 +324,16 @@
             wide = h[c].astype(F32)
             h[c] = (wide * scale_of(wide)).astype(BF)
 
+        after_backward(c)
+
+    def add_terms(m, half):
+        for j in range(ff // 2 // WIDTH):
+            here = pl.ds(j * WIDTH, WIDTH)
+            rows = pl.ds(pl.multiple_of(half * (ff // 2) + j * WIDTH, WIDTH), WIDTH)
+            for lhs, i, total in ((h, 0, tg), (h, 1, tu), (dh, 2, td)):
+                term = sum(dot(lhs[m * per + k], terms[m & 1, i, k, rows, :], NT) for k in range(per))
+                total[half, :, here] += term.astype(BF).astype(F32)
+
     def weights_back(n):
         m, half = n >> 1, n & 1
 
@@ -310,11 +346,7 @@
 
             fetch_terms(m).wait()
 
-        for j in range(ff // 2 // WIDTH):
-            here = pl.ds(pl.multiple_of(half * (ff // 2) + j * WIDTH, WIDTH), WIDTH)
-            for lhs, i, total in ((h, 0, tg), (h, 1, tu), (dh, 2, td)):
-                term = sum(dot(lhs[m * per + k], terms[m & 1, i, k, here, :], NT) for k in range(per))
-                total[:, here] += term.astype(BF).astype(F32)
+        add_terms(m, half)
 
         @pl.when((half == 1) & (m >= later) & (m + 2 < micro))
         def _():
@@ -369,13 +401,17 @@
 
     lax.fori_loop(0, max(len(row) for row in ORDER), word, (jnp.int32(0),) * 5)
 
-    wg[...] = tg[...].astype(BF)
+    cut = ff // 2
+    for i in (0, 1):
+        wg[:, i * cut:(i + 1) * cut] = tg[i].astype(BF)
     out_g = pltpu.make_async_copy(wg, wg_out, w_sem.at[0])
     out_g.start()
-    wu[...] = tu[...].astype(BF)
+    for i in (0, 1):
+        wu[:, i * cut:(i + 1) * cut] = tu[i].astype(BF)
     out_u = pltpu.make_async_copy(wu, wu_out, w_sem.at[1])
     out_u.start()
-    wd[...] = td[...].astype(BF).T
+    for i in (0, 1):
+        wd[i * cut:(i + 1) * cut, :] = td[i].astype(BF).T
     out_d = pltpu.make_async_copy(wd, wd_out, w_sem.at[2])
     out_d.start()
     for copy in (out_g, out_u, out_d):
@@ -422,7 +458,7 @@
             out_specs=[hbm] * 6,
             scratch_shapes=[
                 vmem((d, ff), BF), vmem((d, ff), BF), vmem((ff, d), BF),
-                vmem((d, ff), F32), vmem((d, ff), F32), vmem((d, ff), F32),
+                vmem((2, d, ff // 2), F32), vmem((2, d, ff // 2), F32), vmem((2, d, ff // 2), F32),
                 vmem((chunks, d, T), BF), vmem((chunks, d, T), BF),
                 vmem((4, 2 * ff, T), F32),
                 vmem((RING, 3, per, ff, T), BF), vmem((ff, T), BF),

time: 287 us -> 280 us (0.976)
  Pallas kernels: 279 us -> 272 us
    pallas_call x1, Pallas kernels: 279 us -> 272 us  [step(): pl.pallas_call(functools.partial(kernel, stages), out_shape=(jax.ShapeDty...]
where the time goes in v3:
time: 280 us; the launch traced here: 279 us
  Pallas kernels  272 us (97%)
  local copies, waits for them, and re-layouts  6.61 us (2%)
    pallas_call x1, Pallas kernels, step(): pl.pallas_call(functools.partial(kernel, stages), out_shape=(jax.ShapeDty...  272 us
    unnamed x7, local copies, waits for them, and re-layouts  6.61 us

profile of v3, /device:TPU:0, one launch (start us, length us, event | category | flops | bytes accessed | tf_op | source)
XLA Modules:
  0.0 279.2 jit_solution(3438130710929873892)
XLA Ops:
  0.6 271.9 %shard_map.76 = (bf16[640,1536]{1,0:T(8,128)(2,1)}, bf16[640,1536]{1,0:T(8,128)(2,1)}, bf16[1536,640]{1,0:T(8,128)(2,1)}, f32[32,3072,256]{2,1,0:T(8,128)}, bf16...) custom-call(bf16[16,512,640]{2,1,0:T(8,128)(2,1)} %x.1, bf16[16,512,640]{2,1,0:T(8,128)(2,1)} %dy.1, ...), custom_call_target="tpu_custom_call" | custom-call | tf_op jit(solution)/shard_map/pallas_call | solution.py:447
  272.6 0.0 copy-start.1
  272.6 3.1 %copy.11 = bf16[1,640,1536]{2,1,0:T(8,128)(2,1)} copy(bf16[1,640,1536]{2,1,0:T(8,128)(2,1)} %bitcast.11) | data formatting | bytes 3932160
  275.7 0.0 copy-done.1
  275.7 0.0 copy-start
  275.7 1.3 copy.12
  277.0 1.0 copy-done
  277.9 1.3 copy.13
Async XLA Ops:
  272.6 3.1 %copy-start.1 = (bf16[640,1536]{1,0:T(8,128)(2,1)S(1)}, bf16[640,1536]{1,0:T(8,128)(2,1)}, u32[]{:S(2)}) copy-start(bf16[640,1536]{1,0:T(8,128)(2,1)} %get-tuple-element.7) | copy-start | bytes 5898244
  275.7 2.3 copy-start

commit v4 on v3

--- a/solution.py
+++ b/solution.py
@@ -18,22 +18,22 @@
 RING = 2
 DIGITS = 10
 ORDER = (
-    (153391689, 153391689, 203821641, 176507172, 476398235, 458307794, 461977250, 325662370, 441296090, 325662355, 441296090, 3),
-    (153391689, 153391689, 321720969, 172339849, 304980635, 323597467, 309143251, 457815195, 309143250, 111771),
-    (153391689, 170168905, 423958218, 455647827, 292099786, 458036875, 309143250, 457815195, 309143250, 111771),
-    (153391689, 438866505, 325362889, 442807433, 438871115, 438940299, 457778899, 443131546, 443131546, 111834),
-    (170168905, 155493978, 321492170, 174404249, 174892627, 170435227, 170435227, 306783378, 460175067, 112347),
-    (289706569, 439161947, 189576273, 292074698, 291837521, 455648970, 170435210, 306783370, 460175067, 112347),
-    (291837001, 292135626, 439161499, 290300555, 170202187, 289972874, 289739857, 460137553, 460175067, 112347),
-    (289780817, 191960155, 171029588, 474290394, 292430475, 170440332, 289809034, 289741073, 289739857, 460175067, 898843),
+    (153391689, 153391689, 203821641, 345118793, 457852628, 340899092, 441562267, 325662355, 441296090, 325662355, 441296090, 3),
+    (153391689, 153391689, 438866505, 426058329, 309143250, 457815195, 309143250, 457815195, 309143250, 111771),
+    (153391689, 170168905, 289773137, 321205841, 174891659, 443131091, 323826906, 323826899, 457778323, 112347),
+    (153391689, 287871561, 438638155, 174891722, 423990481, 443130970, 323826906, 323826899, 441300115, 112338),
+    (170168905, 155529818, 325396169, 172275281, 455648969, 170435210, 306783314, 460137618, 460175067, 112347),
+    (289706569, 174367835, 189076555, 156021395, 422094426, 289739929, 306750545, 460137618, 460175067, 112347),
+    (174920777, 289710810, 172298890, 172298890, 289739850, 289739857, 457774161, 460175067, 460175067, 112347),
+    (438875217, 208192603, 292172433, 205853788, 289739874, 170435212, 170435210, 438870666, 462272227, 460175067, 14043),
 )
 
 
-LATER = (16, 16, 16, 16, 8, 8, 6, 8)
-
-
-ON, BY_ON = 0, (8, 9, 10, 11, 12, 14, 16, 18, 20, 22, 23, 25, 28, 30, 31)
-OFF, BY_OFF = 7, (0, 1, 2, 4, 5, 7, 8, 13, 15, 16, 31)
+LATER = (16, 16, 12, 16, 6, 6, 2, 4)
+
+
+ON, BY_ON = 0, (8, 9, 11, 12, 14, 16, 17, 18, 19, 21, 24, 25, 27, 28, 31)
+OFF, BY_OFF = 7, (0, 1, 2, 3, 5, 6, 9, 26, 28)
 
 
 def among(c, chosen):
@@ -79,17 +79,17 @@
 
     def send_y(c):
         return pltpu.make_async_remote_copy(
-            src_ref=y_out.at[c & 1], dst_ref=h.at[c], send_sem=y_send.at[c & 1], recv_sem=y_recv.at[c],
+            src_ref=y_out.at[c & 3], dst_ref=h.at[c], send_sem=y_send.at[c & 3], recv_sem=y_recv.at[c],
             device_id={"pp": right}, device_id_type=MESH)
 
     def send_dh(c):
         return pltpu.make_async_remote_copy(
-            src_ref=dh_out.at[c & 1], dst_ref=dh.at[c], send_sem=dh_send.at[c & 1], recv_sem=dh_recv.at[c],
+            src_ref=dh_out.at[c & 3], dst_ref=dh.at[c], send_sem=dh_send.at[c & 3], recv_sem=dh_recv.at[c],
             device_id={"pp": left}, device_id_type=MESH)
 
     def post_to(source, c, r, target):
         return pltpu.make_async_remote_copy(
-            src_ref=source.at[c & 1], dst_ref=post.at[r], send_sem=(y_send if target == 0 else dh_send).at[c & 1],
+            src_ref=source.at[c & 3], dst_ref=post.at[r], send_sem=(y_send if target == 0 else dh_send).at[c & 3],
             recv_sem=post_recv.at[r], device_id={"pp": target}, device_id_type=MESH)
 
     def post_on(r):
@@ -173,7 +173,7 @@
             if down:
                 pf[here, :] = (gate * jax.nn.sigmoid(gate) * up).astype(BF)
         if down:
-            y_out[c & 1] = h[c] + dot(wd[...], pf[...], TN).astype(BF)
+            y_out[c & 3] = h[c] + dot(wd[...], pf[...], TN).astype(BF)
 
     def before_forward(c, put):
         @pl.when(spill & (c >= 2) & (put == c - 2))
@@ -193,9 +193,9 @@
         def _():
             send_y(c).wait_recv()
 
-        @pl.when((me < last) & (c >= 2))
-        def _():
-            send_y(c - 2).wait_send()
+        @pl.when((me < last) & (c >= 4))
+        def _():
+            send_y(c - 4).wait_send()
 
     def after_forward(c):
         @pl.when(spill)
@@ -255,7 +255,7 @@
         scale = scale_of(wide)
         by_a = (dot(wg[...], terms[at, 0, half]).astype(BF) + dot(wu[...], terms[at, 1, half]).astype(BF)).astype(F32)
         along = jnp.sum(by_a * wide, 0, keepdims=True) * (scale * scale * scale) * (1.0 / d)
-        dh_out[c & 1] = dh[c] + (by_a * scale - wide * along).astype(BF)
+        dh_out[c & 3] = dh[c] + (by_a * scale - wide * along).astype(BF)
         h[c] = (wide * scale).astype(BF)
 
     def before_backward(c, put):
@@ -280,9 +280,9 @@
         def _():
             send_dh(c).wait_recv()
 
-        @pl.when((me > 0) & (c >= 2))
-        def _():
-            send_dh(c - 2).wait_send()
+        @pl.when((me > 0) & (c >= 4))
+        def _():
+            send_dh(c - 4).wait_send()
 
     def after_backward(c):
         @pl.when(((c & 1) == 1) & ((c >> 1) >= later))
@@ -419,12 +419,12 @@
 
     @pl.when(me < last)
     def _():
-        for c in (chunks - 2, chunks - 1):
+        for c in range(chunks - 4, chunks):
             send_y(c).wait_send()
 
     @pl.when(me > 0)
     def _():
-        for c in (chunks - 2, chunks - 1):
+        for c in range(chunks - 4, chunks):
             send_dh(c).wait_send()
 
     def sent(r, _):
@@ -432,6 +432,11 @@
         return 0
 
     lax.fori_loop(0, jnp.where(me == 0, len(BY_ON), jnp.where(me == last, len(BY_OFF), 0)), sent, 0)
+
+
+def hand_out(*refs):
+    for source, target in zip(refs[:3], refs[3:]):
+        target[0] = source[...]
 
 
 def solution(mesh):
@@ -462,12 +467,20 @@
                 vmem((chunks, d, T), BF), vmem((chunks, d, T), BF),
                 vmem((4, 2 * ff, T), F32),
                 vmem((RING, 3, per, ff, T), BF), vmem((ff, T), BF),
-                vmem((2, d, T), BF), vmem((2, d, T), BF), vmem((2, T, d), BF),
-                dma((3,)), dma((2,)), dma((2,)), dma((2,)), dma((2,)), dma((chunks,)), dma((2,)), dma((chunks,)), dma((16,)), dma((16,)), dma((2,)), dma((2,)),
+                vmem((4, d, T), BF), vmem((4, d, T), BF), vmem((2, T, d), BF),
+                dma((3,)), dma((2,)), dma((2,)), dma((2,)), dma((4,)), dma((chunks,)), dma((4,)), dma((chunks,)), dma((16,)), dma((16,)), dma((2,)), dma((2,)),
             ],
             compiler_params=pltpu.CompilerParams(collective_id=0, has_side_effects=True, vmem_limit_bytes=67043328),
         )(x, dy, wg[0], wu[0], wd[0])
-        return tuple(o[None] for o in outs[:3])
+        cut = 2
+        shapes = ((d, ff), (d, ff), (ff, d))
+        return pl.pallas_call(
+            hand_out,
+            grid=(cut,),
+            out_shape=tuple(jax.ShapeDtypeStruct((1, *shape), BF) for shape in shapes),
+            in_specs=[pl.BlockSpec((r // cut, c), lambda i: (i, 0)) for r, c in shapes],
+            out_specs=tuple(pl.BlockSpec((1, r // cut, c), lambda i: (0, i, 0)) for r, c in shapes),
+        )(*outs[:3])
 
     return jax.shard_map(
         step,

time: 280 us -> 275 us (0.982)
  local copies, waits for them, and re-layouts: 6.61 us -> 0 us
    unnamed x7 -> x0, local copies, waits for them, and re-layouts: 6.61 us -> none
    pallas_call x0 -> x1, Pallas kernels: none -> 4.57 us  [step(): pl.pallas_call(hand_out, grid=(cut,), out_shape=tuple((jax.ShapeDtypeStru...]
where the time goes in v4:
time: 275 us
  Pallas kernels  274 us (100%)
    pallas_call x1, Pallas kernels, step(): pl.pallas_call(functools.partial(kernel, stages), out_shape=(jax.ShapeDty...  269 us

profile of v4, /device:TPU:0, one launch (start us, length us, event | category | flops | bytes accessed | tf_op | source)
XLA Modules:
  0.0 274.5 jit_solution(12668600876407932058)
XLA Ops:
  0.6 269.3 %shard_map.76 = (bf16[640,1536]{1,0:T(8,128)(2,1)}, bf16[640,1536]{1,0:T(8,128)(2,1)}, bf16[1536,640]{1,0:T(8,128)(2,1)}, f32[32,3072,256]{2,1,0:T(8,128)}, bf16...) custom-call(bf16[16,512,640]{2,1,0:T(8,128)(2,1)} %x.1, bf16[16,512,640]{2,1,0:T(8,128)(2,1)} %dy.1, ...), custom_call_target="tpu_custom_call" | custom-call | tf_op jit(solution)/shard_map/pallas_call | solution.py:452
  269.9 4.6 %shard_map.77 = (bf16[1,640,1536]{2,1,0:T(8,128)(2,1)}, bf16[1,640,1536]{2,1,0:T(8,128)(2,1)}, bf16[1,1536,640]{2,1,0:T(8,128)(2,1)}) custom-call(bf16[640,1536]{1,0:T(8,128)(2,1)} %get-tuple-element.6.refs_0_, bf16[640,1536]{1,0:T(8,128)(2,1)} %get-tuple-element.7.refs_1_, bf16[1536,640]{1,0:T(8,128)(2,1)} %get-tuple-element.8.refs_2_), custom_call_target="tpu_custom_call" | custom-call | tf_op jit(solution)/shard_map/pallas_call | solution.py:477

commit v5 on v4

--- a/solution.py
+++ b/solution.py
@@ -12,7 +12,7 @@
 NN = (((1,), (0,)), ((), ()))
 NT = (((1,), (1,)), ((), ()))
 TN = (((0,), (0,)), ((), ()))
-FORTH, BACK = 256, 512
+FORTH, BACK = 256, 256
 WIDTH = 256
 T = 256
 RING = 2

time: 275 us -> 274 us (level)
  no operation moved by 1% of the time
where the time goes in v5:
time: 274 us
  Pallas kernels  273 us (100%)
    pallas_call x1, Pallas kernels, step(): pl.pallas_call(functools.partial(kernel, stages), out_shape=(jax.ShapeDty...  268 us

profile of v5, /device:TPU:0, one launch (start us, length us, event | category | flops | bytes accessed | tf_op | source)
XLA Modules:
  0.0 273.6 jit_solution(3775195622708869906)
XLA Ops:
  0.6 268.4 %shard_map.76 = (bf16[640,1536]{1,0:T(8,128)(2,1)}, bf16[640,1536]{1,0:T(8,128)(2,1)}, bf16[1536,640]{1,0:T(8,128)(2,1)}, f32[32,3072,256]{2,1,0:T(8,128)}, bf16...) custom-call(bf16[16,512,640]{2,1,0:T(8,128)(2,1)} %x.1, bf16[16,512,640]{2,1,0:T(8,128)(2,1)} %dy.1, ...), custom_call_target="tpu_custom_call" | custom-call | tf_op jit(solution)/shard_map/pallas_call | solution.py:452
  269.0 4.6 %shard_map.77 = (bf16[1,640,1536]{2,1,0:T(8,128)(2,1)}, bf16[1,640,1536]{2,1,0:T(8,128)(2,1)}, bf16[1,1536,640]{2,1,0:T(8,128)(2,1)}) custom-call(bf16[640,1536]{1,0:T(8,128)(2,1)} %get-tuple-element.6.refs_0_, bf16[640,1536]{1,0:T(8,128)(2,1)} %get-tuple-element.7.refs_1_, bf16[1536,640]{1,0:T(8,128)(2,1)} %get-tuple-element.8.refs_2_), custom_call_target="tpu_custom_call" | custom-call | tf_op jit(solution)/shard_map/pallas_call | solution.py:477
